TPU v7x, 32 devices: a whole 2x2x4 slice. The times are simulated.
32 devices in a mesh: blk: 8 (over z, x), grp: 4 (over y, core).
Axes of the slice: x: 2, y: 2, z: 4, core: 2. Of those that a mesh axis runs over, the one named last changes fastest.
Arguments:
- coil_pos: float32 [3, 1280], P(None, ('blk', 'grp')), may hold values from -1 to 1
- coil_radius: float32 [1280], P(('blk', 'grp')), may hold values from 0.02 to 0.08
- coil_current: bfloat16 [64, 1280], P(None, ('blk', 'grp')), may hold values from -0.3125 to 0.3125
- blank_pos: float32 [3, 4096], P(None, ('blk', 'grp')), may hold values from -1 to 1
- blank_rule: int32 [4096], P(('blk', 'grp')), may hold values from 0 to 7
- blank_cond: float32 [4096], P(('blk', 'grp')), may hold values from 0.3 to 3
- quad_offset: float32 [3, 8, 2], replicated, may hold values from -0.1 to 0.1
- quad_weight: float32 [8, 2], replicated, may hold values from 0.3 to 0.7
Outputs:
- blank_current: bfloat16 [64, 4096], P(None, ('blk', 'grp'))
- coil_reaction: float32 [64, 1280], P(None, ('blk', 'grp'))
All inputs are finite; a program needn't handle non-finite values.
Results may differ from a plain program's by a relative error of at most 0.0066.
Values may be sent and summed in bfloat16 or wider, within the bound.
A program may use at most 64 MiB of HBM per device.

v0:
```python
import math
import jax
import jax.numpy as jnp
from jax import lax
from jax.sharding import PartitionSpec as P


def blank_geometry(blank_pos, blank_rule, quad_offset, quad_weight):
    rules = quad_weight.shape[0]
    points = quad_weight.shape[1]
    onehot = (blank_rule[None, :] == jnp.arange(rules, dtype=jnp.int32)[:, None]).astype(
        jnp.float32
    )
    table_rows = []
    base_rows = []
    zeros_row = jnp.zeros_like(blank_pos[0])
    for point in range(points):
        table_rows += [
            quad_offset[0, :, point],
            quad_offset[1, :, point],
            quad_offset[2, :, point],
            quad_weight[:, point],
        ]
        base_rows += [blank_pos[0], blank_pos[1], blank_pos[2], zeros_row]
    table = jnp.stack(table_rows, 0)
    base = jnp.stack(base_rows, 0)
    return base + jnp.dot(table, onehot, precision=lax.Precision.HIGHEST)


def kernel_block(coil_geometry, geometry):
    points = geometry.shape[0] // 4
    running = jnp.zeros((coil_geometry.shape[1], geometry.shape[1]), jnp.float32)
    for point in range(points):
        delta_x = coil_geometry[0][:, None] - geometry[4 * point][None, :]
        delta_y = coil_geometry[1][:, None] - geometry[4 * point + 1][None, :]
        delta_z = coil_geometry[2][:, None] - geometry[4 * point + 2][None, :]
        squared = (
            delta_x * delta_x + delta_y * delta_y + delta_z * delta_z + coil_geometry[3][:, None]
        )
        running = running + geometry[4 * point + 3][None, :] * lax.rsqrt(squared)
    return running


def blockwise(width, limit, step_fn, initial):
    block = math.gcd(width, limit)
    count = width // block

    def advance(index, carried):
        start = (index * block).astype(jnp.int32)
        return step_fn(carried, start, block)

    return lax.fori_loop(0, count, advance, initial)


def per_device(
    coil_pos, coil_radius, coil_current, blank_pos, blank_rule, blank_cond, quad_offset, quad_weight
):
    coil_geometry = jnp.concatenate([coil_pos, (coil_radius * coil_radius)[None, :]], 0)
    geometry = blank_geometry(blank_pos, blank_rule, quad_offset, quad_weight)
    samples = coil_current.shape[0]
    coil_count = coil_current.shape[1]
    local_blanks = geometry.shape[1]
    total_blanks = local_blanks * lax.axis_size("blk") * lax.axis_size("grp")
    all_current = lax.all_gather(coil_current, ("blk", "grp"), axis=1, tiled=True)
    portion = lax.all_gather(coil_geometry, ("blk", "grp"), axis=1, tiled=True)

    def collect_inner(carried, start, block):
        rows = lax.dynamic_slice_in_dim(portion, start, block, 1)
        kernel_tile = kernel_block(rows, geometry).astype(jnp.bfloat16)
        currents = lax.dynamic_slice_in_dim(all_current, start, block, 1)
        return carried + jnp.dot(currents, kernel_tile, preferred_element_type=jnp.float32)

    induced = blockwise(
        portion.shape[1], 2048, collect_inner, jnp.zeros((samples, local_blanks), jnp.float32)
    )
    blank_current = induced.astype(jnp.bfloat16)
    weighted = (blank_cond[None, :] * blank_current.astype(jnp.float32)).astype(jnp.bfloat16)
    all_weighted = lax.all_gather(weighted, ("blk", "grp"), axis=1, tiled=True)
    reflect_portion = lax.all_gather(geometry, ("blk", "grp"), axis=1, tiled=True)

    def reflect_inner(carried, start, block):
        columns = lax.dynamic_slice_in_dim(reflect_portion, start, block, 1)
        kernel_tile = kernel_block(coil_geometry, columns).astype(jnp.bfloat16)
        currents = lax.dynamic_slice_in_dim(all_weighted, start, block, 1)
        return carried + lax.dot_general(
            currents, kernel_tile, (((1,), (1,)), ((), ())), preferred_element_type=jnp.float32
        )

    reaction = blockwise(
        reflect_portion.shape[1], 2048, reflect_inner, jnp.zeros((samples, coil_count), jnp.float32)
    )
    coil_reaction = reaction * (2.0 / total_blanks)
    return (blank_current, coil_reaction)


def solution(mesh):
    in_specs = (
        P(None, ("blk", "grp")),
        P(("blk", "grp")),
        P(None, ("blk", "grp")),
        P(None, ("blk", "grp")),
        P(("blk", "grp")),
        P(("blk", "grp")),
        P(),
        P(),
    )
    out_specs = (P(None, ("blk", "grp")), P(None, ("blk", "grp")))
    return jax.shard_map(
        per_device, mesh=mesh, in_specs=in_specs, out_specs=out_specs, check_vma=False
    )
```

profile of v0, /device:TPU:0, one launch (start us, length us, event | category | flops | bytes accessed | tf_op | source)
XLA Modules:
  0.0 166.7 jit_solution(2309037192950104632)
XLA Ops:
  0.6 0.0 copy-start.7
  0.6 0.6 copy-done.7
  1.3 0.0 copy-start.4
  1.3 0.7 copy-done.4
  2.0 0.0 copy-start
  2.0 0.0 copy-start.2
  2.0 0.7 copy-done
  2.7 0.0 copy-done.2
  2.7 0.0 copy-start.3
  2.7 0.0 copy-start.6
  2.7 0.6 copy-done.3
  3.4 0.0 copy-done.6
  3.4 0.1 convolution_add_fusion.2
  3.5 43.4 %all-gather = f32[32,40,4]{1,2,0:T(4,128)S(1)} all-gather(f32[1,40,4]{1,2,0:T(4,128)S(1)} %maximum_bitcast_fusion), channel_id=1, replica_groups=mesh['blk'=8,'grp'=4] {'blk','grp'}, dimensions={0}, use_global_device_ids=true | all-gather | bytes 21120 | tf_op jit(solution)/shard_map/all_gather | solution.py:65
  46.9 0.1 reshape.15
  47.0 0.0 copy-start.1
  47.0 37.0 %all_gather.15 = f32[8,4096]{1,0:T(8,128)S(1)} all-gather(f32[8,128]{1,0:T(8,128)S(1)} %convolution_add_fusion.2), channel_id=1, replica_groups=mesh['blk'=8,'grp'=4] {'blk','grp'}, dimensions={1}, use_global_device_ids=true | all-gather | bytes 135168 | tf_op jit(solution)/shard_map/all_gather | solution.py:79
  84.0 0.0 copy-done.1
  84.0 38.8 %all_gather.12 = bf16[64,1280]{0,1:T(8,128)(2,1)S(1)} all-gather(bf16[64,40]{0,1:T(8,128)(2,1)S(1)} %copy-done.1), channel_id=1, replica_groups=mesh['blk'=8,'grp'=4] {'blk','grp'}, dimensions={1}, use_global_device_ids=true | all-gather | bytes 168960 | tf_op jit(solution)/shard_map/all_gather | solution.py:64
  122.9 0.2 copy.14
  123.0 2.3 %while.28 = (s32[]{:T(128)}, f32[64,128]{1,0:T(8,128)S(1)}, bf16[64,1280]{1,0:T(8,128)(2,1)S(1)}, f32[8,128]{1,0:T(8,128)S(1)}, f32[4,1280]{1,0:T(4,128)S(1)}, /...) while((s32[]{:T(128)}, f32[64,128]{1,0:T(8,128)S(1)}, ...), condition=%wide.region_1.0_spmd.clone, body=%wide.region_0.0_spmd.clone.sunk | while | flops 4931594 | bytes 123117 | solution.py:52
  123.1 0.1 constant_dynamic-slice_fusion.3
  123.1 0.3 convolution_add_fusion.5
  123.5 0.1 constant_dynamic-slice_fusion.3
  123.6 0.3 convolution_add_fusion.5
  124.0 0.1 constant_dynamic-slice_fusion.3
  124.1 0.3 convolution_add_fusion.5
  124.4 0.1 constant_dynamic-slice_fusion.3
  124.5 0.3 convolution_add_fusion.5
  124.9 0.1 constant_dynamic-slice_fusion.3
  125.0 0.3 convolution_add_fusion.5
  125.4 0.0 copy-start.5
  125.4 0.6 copy-done.5
  126.0 0.6 multiply_convert_fusion
  126.6 38.0 %all_gather.14 = bf16[64,4096]{1,0:T(8,128)(2,1)S(1)} all-gather(bf16[64,128]{1,0:T(8,128)(2,1)S(1)} %get-tuple-element.278), channel_id=1, replica_groups=mesh['blk'=8,'grp'=4] {'blk','grp'}, dimensions={1}, use_global_device_ids=true | all-gather | bytes 540672 | tf_op jit(solution)/shard_map/all_gather | solution.py:78
  164.7 1.4 while.29
  164.7 0.2 fusion.36
  164.9 0.5 convolution_add_fusion.6
  165.4 0.2 fusion.36
  165.6 0.5 convolution_add_fusion.6
  166.0 0.6 broadcast_multiply_fusion
  (16 shorter events, 0.1 us)
Async XLA Ops:
  0.6 0.7 copy-start.7
  1.3 0.7 copy-start.4
  2.0 0.7 copy-start
  2.0 0.7 copy-start.2
  2.7 0.7 copy-start.3
  2.7 0.7 copy-start.6
  47.0 37.0 %copy-start.1 = (bf16[64,40]{0,1:T(8,128)(2,1)S(1)}, bf16[64,40]{0,1:T(8,128)(2,1)}, u32[]{:S(2)}) copy-start(bf16[64,40]{0,1:T(8,128)(2,1)} %param.14) | copy-start | bytes 15364
  125.4 0.7 copy-start.5
where the time goes:
time: 167 us
  blocking collectives  157 us (94%)
  local copies, waits for them, and re-layouts  4.47 us (3%)
  matrix products  2.78 us (2%)
    all_gather x1, blocking collectives, per_device(): portion = lax.all_gather(coil_geometry, ('blk', 'grp'), axis=1, tiled=True)  43.4 us
    all_gather x1, blocking collectives, per_device(): lax.all_gather(coil_current, ('blk', 'grp'), axis=1, tiled=True)  38.8 us
    all_gather x1, blocking collectives, per_device(): all_weighted = lax.all_gather(weighted, ('blk', 'grp'), axis=1, tiled=True)  38 us
    all_gather x1, blocking collectives, per_device(): lax.all_gather(geometry, ('blk', 'grp'), axis=1, tiled=True)  37 us
    unnamed x18, local copies, waits for them, and re-layouts  3.58 us

commit v1 on v0

--- a/solution.py
+++ b/solution.py
@@ -61,8 +61,16 @@
     coil_count = coil_current.shape[1]
     local_blanks = geometry.shape[1]
     total_blanks = local_blanks * lax.axis_size("blk") * lax.axis_size("grp")
-    all_current = lax.all_gather(coil_current, ("blk", "grp"), axis=1, tiled=True)
-    portion = lax.all_gather(coil_geometry, ("blk", "grp"), axis=1, tiled=True)
+    all_current, portion = jnp.split(
+        lax.all_gather(
+            jnp.concatenate([coil_current, coil_geometry], axis=0),
+            ("blk", "grp"),
+            axis=1,
+            tiled=True,
+        ),
+        [coil_current.shape[0]],
+        axis=0,
+    )
 
     def collect_inner(carried, start, block):
         rows = lax.dynamic_slice_in_dim(portion, start, block, 1)

time: 167 us -> 133 us (0.80)
  blocking collectives: 157 us -> 121 us
  local copies, waits for them, and re-layouts: 4.47 us -> 6.28 us
    all_gather x2 -> x1, blocking collectives: 82.2 us -> 45 us  [per_device(): lax.all_gather(jnp.concatenate([coil_current, coil_geometry], axis=0), ('...]
    unnamed x18 -> x17, local copies, waits for them, and re-layouts: 3.58 us -> 4.27 us
where the time goes in v1:
time: 133 us
  blocking collectives  121 us (91%)
  local copies, waits for them, and re-layouts  6.28 us (5%)
  matrix products  2.77 us (2%)
    all_gather x1, blocking collectives, per_device(): lax.all_gather(jnp.concatenate([coil_current, coil_geometry], axis=0), ('...  45 us
    all_gather x1, blocking collectives, per_device(): lax.all_gather(geometry, ('blk', 'grp'), axis=1, tiled=True)  38.3 us
    all_gather x1, blocking collectives, per_device(): all_weighted = lax.all_gather(weighted, ('blk', 'grp'), axis=1, tiled=True)  38 us
    unnamed x17, local copies, waits for them, and re-layouts  4.27 us

profile of v1, /device:TPU:0, one launch (start us, length us, event | category | flops | bytes accessed | tf_op | source)
XLA Modules:
  0.0 132.6 jit_solution(15322224333912718725)
XLA Ops:
  0.6 0.8 slice_bitcast_fusion.12
  1.4 0.0 copy-start.3
  1.4 0.7 copy-done.3
  2.1 0.0 copy-start.2
  2.1 0.0 copy-start.5
  2.1 0.6 copy-done.2
  2.8 0.0 copy-done.5
  2.8 0.0 copy-start.6
  2.8 0.1 convolution_add_fusion.2
  2.9 0.5 copy-done.6
  3.4 0.0 copy-start.1
  3.4 0.1 copy.12
  3.5 0.6 copy-done.1
  4.1 0.0 copy-start
  4.1 0.7 copy-done
  4.8 0.1 copy.11
  4.9 0.1 pad_maximum_fusion
  5.0 45.0 %all_gather.9 = f32[68,1280]{0,1:T(8,128)S(1)} all-gather(f32[68,40]{0,1:T(8,128)S(1)} %pad_maximum_fusion), channel_id=1, replica_groups=mesh['blk'=8,'grp'=4] {'blk','grp'}, dimensions={1}, use_global_device_ids=true | all-gather | bytes 359040 | tf_op jit(solution)/shard_map/all_gather | solution.py:65
  50.0 0.2 split.9
  50.2 0.2 copy.14
  50.5 0.2 copy.13
  50.7 2.3 %while.28 = (s32[]{:T(128)}, f32[64,128]{1,0:T(8,128)S(1)}, bf16[64,1280]{1,0:T(8,128)(2,1)S(1)}, f32[8,128]{1,0:T(8,128)S(1)}, f32[4,1280]{1,0:T(4,128)S(1)}, /...) while((s32[]{:T(128)}, f32[64,128]{1,0:T(8,128)S(1)}, ...), condition=%wide.region_1.0_spmd.clone, body=%wide.region_0.0_spmd.clone.sunk | while | flops 4931594 | bytes 123109 | solution.py:52
  50.7 0.1 constant_dynamic-slice_fusion.3
  50.8 0.3 convolution_add_fusion.5
  51.2 0.1 constant_dynamic-slice_fusion.3
  51.3 0.3 convolution_add_fusion.5
  51.6 0.1 constant_dynamic-slice_fusion.3
  51.7 0.3 convolution_add_fusion.5
  52.1 0.1 constant_dynamic-slice_fusion.3
  52.2 0.3 convolution_add_fusion.5
  52.6 0.1 constant_dynamic-slice_fusion.3
  52.7 0.3 convolution_add_fusion.5
  53.0 0.0 copy-start.4
  53.0 0.6 copy-done.4
  53.7 0.6 multiply_convert_fusion
  54.3 38.0 %all_gather.10 = bf16[64,4096]{1,0:T(8,128)(2,1)S(1)} all-gather(bf16[64,128]{1,0:T(8,128)(2,1)S(1)} %get-tuple-element.273), channel_id=1, replica_groups=mesh['blk'=8,'grp'=4] {'blk','grp'}, dimensions={1}, use_global_device_ids=true | all-gather | bytes 540672 | tf_op jit(solution)/shard_map/all_gather | solution.py:86
  92.3 38.3 %all_gather.11 = f32[8,4096]{1,0:T(8,128)S(1)} all-gather(f32[8,128]{1,0:T(8,128)S(1)} %get-tuple-element.509), channel_id=1, replica_groups=mesh['blk'=8,'grp'=4] {'blk','grp'}, dimensions={1}, use_global_device_ids=true | all-gather | bytes 135168 | tf_op jit(solution)/shard_map/all_gather | solution.py:87
  130.6 1.4 %while.29 = (s32[]{:T(128)}, f32[64,40]{0,1:T(8,128)S(1)}, bf16[64,4096]{1,0:T(8,128)(2,1)S(1)}, f32[8,4096]{1,0:T(8,128)S(1)}, f32[3,40]{1,0:T(4,128)S(1)}, /*i...) while((s32[]{:T(128)}, f32[64,40]{0,1:T(8,128)S(1)}, ...), condition=%wide.region_3.0_spmd.clone, body=%wide.region_2.0_spmd.clone.sunk | while | flops 12293134 | bytes 492813 | solution.py:52
  130.6 0.2 fusion.36
  130.8 0.5 convolution_add_fusion.6
  131.3 0.2 fusion.36
  131.5 0.5 convolution_add_fusion.6
  132.0 0.6 broadcast_multiply_fusion
  (15 shorter events, 0.1 us)
Async XLA Ops:
  1.4 0.7 copy-start.3
  2.1 0.7 copy-start.2
  2.1 0.7 copy-start.5
  2.8 0.7 copy-start.6
  3.4 0.7 copy-start.1
  4.1 0.7 copy-start
  53.0 0.7 copy-start.4
